TPU v7x, 32 devices: a whole 2x2x4 slice. The times are simulated.
32 devices in a mesh: seq: 8 (over z, y), head: 4 (over x, core).
Axes of the slice: x: 2, y: 2, z: 4, core: 2. Of those that a mesh axis runs over, the one named last changes fastest.
Arguments:
- queries: bfloat16 [4096, 12288], P(('seq', 'head')), may hold values from -8 to 8
- latent: bfloat16 [4096, 512], P(('seq', 'head')), may hold values from -6 to 6
- rope_keys: bfloat16 [4096, 64], P(('seq', 'head')), may hold values from -8 to 8
- key_weight: bfloat16 [512, 8192], P('seq', 'head'), may hold values from -0.25 to 0.25
- value_weight: bfloat16 [512, 8192], P('seq', 'head'), may hold values from -0.25 to 0.25
- doc_lengths: int32 [32], replicated, may hold values from 1 to 254, as said below
Outputs:
- attended: bfloat16 [4096, 8192], P(('seq', 'head'))
Inputs may be any that keep to these rules, and one draw needn't show every extreme that they name: `doc_lengths`: the documents lie in order in the pack and their lengths sum to 4096; document 0 starts at position 0 and every other document d starts strictly inside positions d * 128 to (d + 1) * 128 - 1, excluding the first of these; one length is exactly 254.
All inputs are finite; a program needn't handle non-finite values.
Results may differ from a plain program's by a relative error of at most 0.0062.
Values may be sent and summed in bfloat16 or wider, within the bound.
A program may use at most 128 MiB of HBM per device.

v0:
```python
import math
import jax
import jax.numpy as jnp
from jax import lax
from jax.sharding import PartitionSpec as P

NOPE = 128
ROPE = 64
VDIM = 128
lowest_score = -1e30


def shifted(value, axis, steps):
    count = lax.axis_size(axis)
    first, last = (max(0, -steps), min(count, count - steps))
    return lax.ppermute(value, axis, [(source, source + steps) for source in range(first, last)])


def document_of(doc_lengths, first_place, count):
    starts = jnp.cumsum(doc_lengths) - doc_lengths
    places = first_place + jnp.arange(count, dtype=jnp.int32)
    started = (starts[None, :] <= places[:, None]).astype(jnp.int32)
    return jnp.sum(started, axis=1) - 1


def shards(queries, latent, rope_keys, key_weight, value_weight, doc_lengths):
    tok_rows = queries.shape[0]
    groups = lax.axis_size("head")
    group_rows = tok_rows * groups
    local_heads = key_weight.shape[1] // NOPE
    qk_width = NOPE + ROPE
    block_rows = min(512, group_rows)
    score_scale = 1.0 / math.sqrt(qk_width)
    group_latent, group_rope = (
        lax.all_gather(latent, "head", axis=0, tiled=True),
        lax.all_gather(rope_keys, "head", axis=0, tiled=True),
    )
    by_heads = queries.reshape(tok_rows, groups, local_heads * qk_width)
    my_queries = lax.all_to_all(by_heads, "head", split_axis=1, concat_axis=0, tiled=True)
    my_queries = my_queries.reshape(group_rows, local_heads, qk_width)
    earlier_latent, earlier_rope = shifted((group_latent, group_rope), "seq", 1)
    latent_rows = jnp.concatenate([earlier_latent, group_latent], axis=0)
    key_sums = jnp.dot(
        latent_rows,
        lax.all_gather(key_weight, "seq", axis=0, tiled=True),
        preferred_element_type=jnp.float32,
    )
    value_sums = jnp.dot(
        latent_rows,
        lax.all_gather(value_weight, "seq", axis=0, tiled=True),
        preferred_element_type=jnp.float32,
    )
    keys_all = key_sums.astype(jnp.bfloat16)
    values_all = value_sums.astype(jnp.bfloat16)
    rope_all = jnp.concatenate([earlier_rope, group_rope], axis=0)
    first_place = lax.axis_index("seq") * group_rows - group_rows
    key_docs = document_of(doc_lengths, first_place, 2 * group_rows)
    key_blocks = group_rows // block_rows + 1

    def one_block(q_index):
        q_start = q_index * block_rows
        q_block = lax.dynamic_slice_in_dim(my_queries, q_start, block_rows, 0)
        q_nope = q_block[:, :, :NOPE]
        q_rope = q_block[:, :, NOPE:]
        q_docs = lax.dynamic_slice_in_dim(key_docs, group_rows + q_start, block_rows, 0)
        q_places = group_rows + q_start + jnp.arange(block_rows, dtype=jnp.int32)

        def attend(state_now, k_start):
            row_peak, row_sum, weighted = state_now
            k_nope = lax.dynamic_slice_in_dim(keys_all, k_start, block_rows, 0).reshape(
                block_rows, local_heads, NOPE
            )
            k_rope = lax.dynamic_slice_in_dim(rope_all, k_start, block_rows, 0)
            k_values = lax.dynamic_slice_in_dim(values_all, k_start, block_rows, 0).reshape(
                block_rows, local_heads, VDIM
            )
            k_docs = lax.dynamic_slice_in_dim(key_docs, k_start, block_rows, 0)
            k_places = k_start + jnp.arange(block_rows, dtype=jnp.int32)
            scores = jnp.einsum("ihd,jhd->hij", q_nope, k_nope, preferred_element_type=jnp.float32)
            scores = (
                scores
                + jnp.einsum("ihd,jd->hij", q_rope, k_rope, preferred_element_type=jnp.float32)
            ) * score_scale
            allowed = (q_docs[:, None] == k_docs[None, :]) & (
                k_places[None, :] <= q_places[:, None]
            )
            scores = jnp.where(allowed[None, :, :], scores, -jnp.inf)
            new_peak = jnp.maximum(row_peak, jnp.max(scores, axis=2))
            expo = jnp.exp(scores - new_peak[:, :, None])
            rescale = jnp.exp(row_peak - new_peak)
            row_sum = row_sum * rescale + jnp.sum(expo, axis=2)
            rounded = expo.astype(jnp.bfloat16)
            weighted = weighted * jnp.transpose(rescale)[:, :, None] + jnp.einsum(
                "hij,jhd->ihd", rounded, k_values, preferred_element_type=jnp.float32
            )
            return (new_peak, row_sum, weighted)

        def visit(k_index, state_now):
            k_start = (q_index + k_index) * block_rows
            return attend(state_now, k_start)

        start_state = (
            jnp.full((local_heads, block_rows), lowest_score, jnp.float32),
            jnp.zeros((local_heads, block_rows), jnp.float32),
            jnp.zeros((block_rows, local_heads, VDIM), jnp.float32),
        )
        row_peak, row_sum, weighted = lax.fori_loop(0, key_blocks, visit, start_state)
        mixed = weighted / jnp.transpose(row_sum)[:, :, None]
        return mixed.reshape(block_rows, local_heads * VDIM).astype(jnp.bfloat16)

    attended = lax.map(one_block, jnp.arange(group_rows // block_rows, dtype=jnp.int32))
    attended = attended.reshape(group_rows, local_heads * VDIM)
    return lax.all_to_all(attended, "head", split_axis=0, concat_axis=1, tiled=True)


def solution(mesh):
    placed = (
        P(("seq", "head"), None),
        P(("seq", "head"), None),
        P(("seq", "head"), None),
        P("seq", "head"),
        P("seq", "head"),
        P(),
    )
    return jax.shard_map(
        shards, mesh=mesh, in_specs=placed, out_specs=P(("seq", "head"), None), check_vma=False
    )
```

profile of v0, /device:TPU:24, one launch (start us, length us, event | category | flops | bytes accessed | tf_op | source)
XLA Modules:
  0.0 263.6 jit_solution(16397362102744043481)
XLA Ops:
  6.5 0.7 all-gather.5.cloned.1.call-update
  7.3 0.0 all-gather.3.cloned.1.call-start
  7.3 0.7 all-gather.3.cloned.1.call-update
  8.0 4.7 %copy.43 = bf16[128,12288]{0,1:T(8,128)(2,1)} copy(bf16[128,12288]{1,0:T(8,128)(2,1)} %param.8) | data formatting | bytes 6291456 | tf_op args[0]
  12.7 3.8 %all-to-all-start = ((bf16[128,4,3072]{0,2,1:T(8,128)(2,1)}), bf16[128,4,3072]{0,2,1:T(8,128)(2,1)S(1)}, u32[]{:S(2)}, u32[]{:S(2)}) async-start(bf16[128,4,3072]{0,2,1:T(8,128)(2,1)} %bitcast.61), calls=%async_computation | async-start | bytes 6291456 | tf_op jit(solution)/shard_map/all_to_all | solution.py:39
  16.5 41.0 %all_gather.12 = bf16[512,512]{1,0:T(8,128)(2,1)} all-gather(bf16[128,512]{1,0:T(8,128)(2,1)S(1)} %copy-done), channel_id=1, replica_groups=mesh['seq'=8,'head'=4] {'head'}, dimensions={0}, use_global_device_ids=true | all-gather | bytes 655360 | tf_op jit(solution)/shard_map/all_gather | solution.py:35
  57.5 3.4 %collective-permute-start = (bf16[512,512]{1,0:T(8,128)(2,1)}, bf16[512,512]{1,0:T(8,128)(2,1)}, u32[]{:S(2)}, u32[]{:S(2)}) collective-permute-start(bf16[512,512]{1,0:T(8,128)(2,1)} %all_gather.12), channel_id=1, source_target_pairs={{0,4},{4,8},{8,12},{12,16},{16,20},{20,24},{24,28},{1,5},{5,9},{9,... | collective-permute-start | bytes 1572872 | tf_op jit(solution)/shard_map/ppermute | solution.py:16
  60.9 5.3 %all_gather.14 = bf16[512,64]{0,1:T(8,128)(2,1)S(1)} all-gather(bf16[128,64]{0,1:T(8,128)(2,1)S(1)} %copy-done.1), channel_id=1, replica_groups=mesh['seq'=8,'head'=4] {'head'}, dimensions={0}, use_global_device_ids=true | all-gather | bytes 81920 | tf_op jit(solution)/shard_map/all_gather | solution.py:36
  66.2 1.9 collective-permute-start.1
  68.1 0.1 copy.42
  68.2 0.1 reduce-window.9
  68.3 0.1 reduce
  68.4 0.1 convert_reduce_fusion
  68.6 15.9 %collective-permute-done.1 = bf16[512,64]{0,1:T(8,128)(2,1)S(1)} collective-permute-done((bf16[512,64]{0,1:T(8,128)(2,1)S(1)}, bf16[512,64]{0,1:T(8,128)(2,1)S(1)}, u32[]{:S(2)}, u32[]{:S(2)}) %collective-permute-start.1) | collective-permute-done | bytes 65568 | tf_op jit(solution)/shard_map/ppermute | solution.py:16
  84.5 1.9 constant_dynamic-update-slice_fusion.1
  86.4 1.9 constant_dynamic-update-slice_fusion
  88.3 15.6 %copy.44 = bf16[4,128,1,3072]{1,0,3,2:T(4,128)(2,1)} copy(bf16[4,128,1,3072]{1,3,0,2:T(8,128)(2,1)S(1)} %bitcast.60) | data formatting | bytes 6291456 | tf_op jit(solution)/shard_map/all_to_all | solution.py:39
  103.9 4.0 %reshape.132 = bf16[512,16,192]{0,2,1:T(8,128)(2,1)S(1)} reshape(bf16[4,128,1,3072]{1,0,3,2:T(4,128)(2,1)} %copy.44) | data formatting | bytes 6291456 | tf_op jit(solution)/shard_map/reshape | solution.py:40
  107.9 1.5 slice.11
  109.4 1.1 slice.12
  110.5 3.9 %copy.46 = bf16[512,16,128]{2,0,1:T(8,128)(2,1)} copy(bf16[512,16,128]{0,2,1:T(8,128)(2,1)} %slice.11) | data formatting | bytes 4194304
  114.4 6.2 %convolution_convert_fusion = bf16[1024,2048]{1,0:T(8,128)(2,1)} fusion(bf16[1024,512]{1,0:T(8,128)(2,1)} %constant_dynamic-update-slice_fusion, bf16[512,2048]{1,0:T(8,128)(2,1)} %all-gather.5.cloned.1.call-done), kind=kOutput, calls=%fused_computation.25 | convolution fusion | flops 2149580800 | bytes 7340032 | tf_op jit(solution)/shard_map/dot_general | solution.py:48
  120.6 6.2 %convolution_convert_fusion.1 = bf16[1024,2048]{1,0:T(8,128)(2,1)} fusion(bf16[1024,512]{1,0:T(8,128)(2,1)} %constant_dynamic-update-slice_fusion, bf16[512,2048]{1,0:T(8,128)(2,1)} %all-gather.3.cloned.1.call-done), kind=kOutput, calls=%fused_computation.26 | convolution fusion | flops 2149580800 | bytes 7340032 | tf_op jit(solution)/shard_map/dot_general | solution.py:43
  126.8 87.3 %while.27 = (s32[]{:T(128)}, f32[16,512]{1,0:T(8,128)S(1)}, f32[16,512]{1,0:T(8,128)S(1)}, f32[512,16,128]{0,2,1:T(8,128)}, s32[512]{0:T(512)S(1)}, /*index=5*/s...) while((s32[]{:T(128)}, f32[16,512]{1,0:T(8,128)S(1)}, ...), condition=%wide.region_5.6_spmd.clone, body=%wide.region_2.5_spmd.clone.sunk | while | flops 2721891328 | bytes 117522640 | solution.py:107
  126.8 0.1 dynamic_slice.63
  126.9 0.3 compare_and_fusion.2
  127.2 4.8 %constant_dynamic-slice_fusion.3 = (bf16[512,2048]{1,0:T(8,128)(2,1)}, bf16[512,2048]{1,0:T(8,128)(2,1)}) fusion(bf16[1024,2048]{1,0:T(8,128)(2,1)} %get-tuple-element.540, s32[]{:T(128)S(6)} %select_n.30, bf16[1024,2048]{1,0:T(8,128)(2,1)} %get-tuple-element.536), kind=kLoop, calls=%fused_computation.21.clone.1 | loop fusion | bytes 8388612 | tf_op jit(solution)/shard_map/while/body/eval_jaxpr/while/body/eval_jaxpr/dynamic_slice | solution.py:74
  132.1 2.9 %copy.58 = bf16[512,2048]{0,1:T(8,128)(2,1)S(1)} copy(bf16[512,2048]{1,0:T(8,128)(2,1)} %get-tuple-element.492) | data formatting | bytes 4194304 | tf_op jit(solution)/shard_map/while/body/eval_jaxpr/while/body/eval_jaxpr/dynamic_slice | solution.py:70
  134.9 4.0 %fusion.41 = f32[16,512,512]{2,1,0:T(8,128)S(1)} fusion(bf16[512,16,128]{0,2,1:T(8,128)(2,1)S(1)} %bitcast.59, bf16[512,16,128]{2,0,1:T(8,128)(2,1)} %get-tuple-element.537), kind=kOutput, calls=%fused_computation.34.clone.1 | convolution fusion | flops 1073741824 | bytes 20971520 | tf_op jit(solution)/shard_map/while/body/eval_jaxpr/while/body/eval_jaxpr/ihd,jhd->hij/dot_general | solution.py:79
  138.9 9.0 %fusion.42 = (f32[16,512]{1,0:T(8,128)S(1)}, f32[16,512,512]{1,2,0:T(8,128)}) fusion(bf16[512,16,64]{0,2,1:T(8,128)(2,1)} %get-tuple-element.539, bf16[1024,64]{0,1:T(8,128)(2,1)S(1)} %get-tuple-element.538, s32[]{:T(128)S(6)} %select_n.30, f32[16,512,512]{2,1,0:T(8,128)S(1)} %fusion.41, pred[512,512]{0,1:T(8,128)(4,1)S(1)} %compare_and_fusion.2), kind=kOutput, calls=%fused_computation.33.clone.1 | convolution fusion | flops 553639936 | bytes 34963460 | tf_op jit(solution)/shard_map/while/body/eval_jaxpr/while/body/eval_jaxpr/ihd,jd->hij/dot_general | solution.py:82
  147.9 2.9 %copy.59 = bf16[512,2048]{0,1:T(8,128)(2,1)S(1)} copy(bf16[512,2048]{1,0:T(8,128)(2,1)} %get-tuple-element.498) | data formatting | bytes 4194304 | tf_op jit(solution)/shard_map/while/body/eval_jaxpr/while/body/eval_jaxpr/dynamic_slice | solution.py:74
  150.8 10.8 %bitcast_add_fusion.3 = f32[512,16,128]{0,2,1:T(8,128)} fusion(f32[512,16,128]{0,2,1:T(8,128)} %get-tuple-element.518, bf16[512,16,128]{0,2,1:T(8,128)(2,1)S(1)} %bitcast.58, f32[16,512,512]{1,2,0:T(8,128)} %get-tuple-element.497, f32[16,512]{1,0:T(8,128)S(1)} %get-tuple-element.531, f32[512,16]{0,1:T(8,128)S(1)} %get-tuple-element.499, pred[]{:T(512)S(6)} %compare.3), kind=kOutput, calls=%fused_computation.9.clone.1 | convolution fusion | flops 1085276160 | bytes 27328512 | tf_op jit(solution)/shard_map/while/body/eval_jaxpr/while/body/eval_jaxpr/hij,jhd->ihd/dot_general | solution.py:93
  161.6 8.3 %fusion.44 = f32[16,512]{1,0:T(8,128)S(1)} fusion(f32[16,512,512]{1,2,0:T(8,128)} %get-tuple-element.497, f32[16,512]{1,0:T(8,128)S(1)} %get-tuple-element.531), kind=kLoop, calls=%fused_computation.6.clone.1 | loop fusion | flops 8380416 | bytes 16842752 | tf_op jit(solution)/shard_map/while/body/eval_jaxpr/while/body/eval_jaxpr/reduce_sum | solution.py:91
  169.9 0.1 dynamic_slice.63
  170.0 0.3 compare_and_fusion.2
  170.3 4.8 %constant_dynamic-slice_fusion.3 = (bf16[512,2048]{1,0:T(8,128)(2,1)}, bf16[512,2048]{1,0:T(8,128)(2,1)}) fusion(bf16[1024,2048]{1,0:T(8,128)(2,1)} %get-tuple-element.540, s32[]{:T(128)S(6)} %select_n.30, bf16[1024,2048]{1,0:T(8,128)(2,1)} %get-tuple-element.536), kind=kLoop, calls=%fused_computation.21.clone.1 | loop fusion | bytes 8388612 | tf_op jit(solution)/shard_map/while/body/eval_jaxpr/while/body/eval_jaxpr/dynamic_slice | solution.py:74
  175.1 2.9 %copy.58 = bf16[512,2048]{0,1:T(8,128)(2,1)S(1)} copy(bf16[512,2048]{1,0:T(8,128)(2,1)} %get-tuple-element.492) | data formatting | bytes 4194304 | tf_op jit(solution)/shard_map/while/body/eval_jaxpr/while/body/eval_jaxpr/dynamic_slice | solution.py:70
  178.0 4.0 %fusion.41 = f32[16,512,512]{2,1,0:T(8,128)S(1)} fusion(bf16[512,16,128]{0,2,1:T(8,128)(2,1)S(1)} %bitcast.59, bf16[512,16,128]{2,0,1:T(8,128)(2,1)} %get-tuple-element.537), kind=kOutput, calls=%fused_computation.34.clone.1 | convolution fusion | flops 1073741824 | bytes 20971520 | tf_op jit(solution)/shard_map/while/body/eval_jaxpr/while/body/eval_jaxpr/ihd,jhd->hij/dot_general | solution.py:79
  182.0 9.0 %fusion.42 = (f32[16,512]{1,0:T(8,128)S(1)}, f32[16,512,512]{1,2,0:T(8,128)}) fusion(bf16[512,16,64]{0,2,1:T(8,128)(2,1)} %get-tuple-element.539, bf16[1024,64]{0,1:T(8,128)(2,1)S(1)} %get-tuple-element.538, s32[]{:T(128)S(6)} %select_n.30, f32[16,512,512]{2,1,0:T(8,128)S(1)} %fusion.41, pred[512,512]{0,1:T(8,128)(4,1)S(1)} %compare_and_fusion.2), kind=kOutput, calls=%fused_computation.33.clone.1 | convolution fusion | flops 553639936 | bytes 34963460 | tf_op jit(solution)/shard_map/while/body/eval_jaxpr/while/body/eval_jaxpr/ihd,jd->hij/dot_general | solution.py:82
  190.9 2.9 %copy.59 = bf16[512,2048]{0,1:T(8,128)(2,1)S(1)} copy(bf16[512,2048]{1,0:T(8,128)(2,1)} %get-tuple-element.498) | data formatting | bytes 4194304 | tf_op jit(solution)/shard_map/while/body/eval_jaxpr/while/body/eval_jaxpr/dynamic_slice | solution.py:74
  193.8 12.0 %bitcast_add_fusion.3 = f32[512,16,128]{0,2,1:T(8,128)} fusion(f32[512,16,128]{0,2,1:T(8,128)} %get-tuple-element.518, bf16[512,16,128]{0,2,1:T(8,128)(2,1)S(1)} %bitcast.58, f32[16,512,512]{1,2,0:T(8,128)} %get-tuple-element.497, f32[16,512]{1,0:T(8,128)S(1)} %get-tuple-element.531, f32[512,16]{0,1:T(8,128)S(1)} %get-tuple-element.499, pred[]{:T(512)S(6)} %compare.3), kind=kOutput, calls=%fused_computation.9.clone.1 | convolution fusion | flops 1085276160 | bytes 27328512 | tf_op jit(solution)/shard_map/while/body/eval_jaxpr/while/body/eval_jaxpr/hij,jhd->ihd/dot_general | solution.py:93
  205.8 8.3 %fusion.44 = f32[16,512]{1,0:T(8,128)S(1)} fusion(f32[16,512,512]{1,2,0:T(8,128)} %get-tuple-element.497, f32[16,512]{1,0:T(8,128)S(1)} %get-tuple-element.531), kind=kLoop, calls=%fused_computation.6.clone.1 | loop fusion | flops 8380416 | bytes 16842752 | tf_op jit(solution)/shard_map/while/body/eval_jaxpr/while/body/eval_jaxpr/reduce_sum | solution.py:91
  214.1 2.8 %divide_convert_fusion = bf16[512,16,128]{0,2,1:T(8,128)(2,1)S(1)} fusion(f32[512,16,128]{0,2,1:T(8,128)} %get-tuple-element.292, f32[512,16]{0,1:T(8,128)S(1)} %bitcast.63), kind=kLoop, calls=%fused_computation.24 | loop fusion | flops 2097152 | bytes 6324224 | tf_op jit(solution)/shard_map/while/body/eval_jaxpr/convert_element_type | solution.py:109
  216.9 2.0 reshape.136
  219.0 3.0 %copy.53 = bf16[4,128,2048]{2,1,0:T(8,128)(2,1)S(1)} copy(bf16[4,128,2048]{1,0,2:T(4,128)(2,1)} %reshape.136) | data formatting | bytes 4194304 | tf_op jit(solution)/shard_map/while/body/eval_jaxpr/convert_element_type | solution.py:109
  221.9 28.9 %all_to_all.31 = bf16[4,128,2048]{2,1,0:T(8,128)(2,1)} all-to-all(bf16[4,128,2048]{2,1,0:T(8,128)(2,1)S(1)} %copy.53), channel_id=1, replica_groups=mesh['seq'=8,'head'=4] {'head'}, dimensions={0} | all-to-all | bytes 4194304 | tf_op jit(solution)/shard_map/all_to_all | solution.py:113
  250.8 3.0 %copy.49 = bf16[4,128,2048]{1,2,0:T(8,128)(2,1)S(1)} copy(bf16[4,128,2048]{2,1,0:T(8,128)(2,1)} %all_to_all.31) | data formatting | bytes 4194304 | tf_op jit(solution)/shard_map/all_to_all | solution.py:113
  253.9 2.9 %copy.50 = bf16[128,8192]{1,0:T(8,128)(2,1)} copy(bf16[128,8192]{0,1:T(8,128)(2,1)S(1)} %bitcast.62) | data formatting | bytes 4194304 | tf_op jit(solution)/shard_map/all_to_all | solution.py:113
  (27 shorter events, 0.1 us)
Async XLA Ops:
  6.5 107.9 %all-gather.5.cloned.1.call-start = ((), (), s32[]{:S(2)}) async-start(), calls=%async_computation.3 | async-start | bytes 2359296 | tf_op jit(solution)/shard_map/all_gather | solution.py:50
  7.3 113.4 %all-gather.3.cloned.1.call-start = ((), (), s32[]{:S(2)}) async-start(), calls=%async_computation.2 | async-start | bytes 2359296 | tf_op jit(solution)/shard_map/all_gather | solution.py:45
  12.7 3.9 %copy-start = (bf16[128,512]{1,0:T(8,128)(2,1)S(1)}, bf16[128,512]{1,0:T(8,128)(2,1)}, u32[]{:S(2)}) copy-start(bf16[128,512]{1,0:T(8,128)(2,1)} %param.9) | copy-start | bytes 393220
  12.7 48.3 %copy-start.1 = (bf16[128,64]{0,1:T(8,128)(2,1)S(1)}, bf16[128,64]{0,1:T(8,128)(2,1)}, u32[]{:S(2)}) copy-start(bf16[128,64]{0,1:T(8,128)(2,1)} %param.10) | copy-start | bytes 49156
  12.7 55.5 %copy-start.2 = (s32[32]{0:T(128)S(1)}, s32[32]{0:T(128)}, u32[]{:S(2)}) copy-start(s32[32]{0:T(128)} %param.13) | copy-start | bytes 388
  12.7 75.6 %all-to-all-start = ((bf16[128,4,3072]{0,2,1:T(8,128)(2,1)}), bf16[128,4,3072]{0,2,1:T(8,128)(2,1)S(1)}, u32[]{:S(2)}, u32[]{:S(2)}) async-start(bf16[128,4,3072]{0,2,1:T(8,128)(2,1)} %bitcast.61), calls=%async_computation | async-start | bytes 6291456 | tf_op jit(solution)/shard_map/all_to_all | solution.py:39
  57.5 27.0 %collective-permute-start = (bf16[512,512]{1,0:T(8,128)(2,1)}, bf16[512,512]{1,0:T(8,128)(2,1)}, u32[]{:S(2)}, u32[]{:S(2)}) collective-permute-start(bf16[512,512]{1,0:T(8,128)(2,1)} %all_gather.12), channel_id=1, source_target_pairs={{0,4},{4,8},{8,12},{12,16},{16,20},{20,24},{24,28},{1,5},{5,9},{9,... | collective-permute-start | bytes 1572872 | tf_op jit(solution)/shard_map/ppermute | solution.py:16
  66.2 18.3 %collective-permute-start.1 = (bf16[512,64]{0,1:T(8,128)(2,1)S(1)}, bf16[512,64]{0,1:T(8,128)(2,1)S(1)}, u32[]{:S(2)}, u32[]{:S(2)}) collective-permute-start(bf16[512,64]{0,1:T(8,128)(2,1)S(1)} %all_gather.14), channel_id=1, source_target_pairs={{0,4},{4,8},{8,12},{12,16},{16,20},{20,24},{24,28},{1,5},{5,9},{9,... | collective-permute-start | bytes 196616 | tf_op jit(solution)/shard_map/ppermute | solution.py:16
Sparse Core Ops, SparseCore 0:
  9.5 48.5 all-gather.4
  60.2 50.0 all-gather.2
where the time goes:
time: 265 us; the launch traced here: 264 us
  blocking collectives  75.1 us (28%)
  local copies, waits for them, and re-layouts  66.8 us (25%)
  matrix products  61.1 us (23%)
  other arithmetic  20.3 us (8%)
  waiting for transfers between devices  17.4 us (7%)
  between operations  13.6 us (5%)
  starting transfers between devices  9.2 us (3%)
    all_gather x1, blocking collectives, shards(): lax.all_gather(latent, 'head', axis=0, tiled=True)  41 us
    all_to_all x1, blocking collectives, shards(): lax.all_to_all(attended, 'head', split_axis=0, concat_axis=1, tiled=True)  28.9 us
    dot_general x2, matrix products, attend(): jnp.einsum('hij,jhd->ihd', rounded, k_values, preferred_element_type=jnp....  22.8 us
    dot_general x2, matrix products, attend(): jnp.einsum('ihd,jd->hij', q_rope, k_rope, preferred_element_type=jnp.floa...  18 us
    reduce_sum x2, other arithmetic, attend(): row_sum = row_sum * rescale + jnp.sum(expo, axis=2)  16.5 us
    ppermute x2, waiting for transfers between devices, shifted(): lax.ppermute(value, axis, [(source, source + steps) for source in range(f...  15.9 us
    all_to_all x1, local copies, waits for them, and re-layouts, shards(): lax.all_to_all(by_heads, 'head', split_axis=1, concat_axis=0, tiled=True)  15.6 us
    dynamic_slice x4, local copies, waits for them, and re-layouts, attend(): lax.dynamic_slice_in_dim(values_all, k_start, block_rows, 0)  15.4 us
  transfers between devices with their start and end apart: 5, of which 1 were waited for; matrix products, arithmetic and copies ran while one was open for 16% of the time, Pallas kernels for 0%

commit v1 on v0

--- a/solution.py
+++ b/solution.py
@@ -8,6 +8,23 @@
 ROPE = 64
 VDIM = 128
 lowest_score = -1e30
+
+
+def in_order(blocks, dim):
+    dims = list(blocks.shape[1:])
+    dims[dim] *= blocks.shape[0]
+    return jnp.moveaxis(blocks, 0, dim).reshape(dims)
+
+
+def collect(x, axis, dim):
+    size = lax.axis_size(axis)
+    ahead = [(i, (i + 1) % size) for i in range(size)]
+    tiles = [x]
+    while len(tiles) < size:
+        tiles.append(lax.ppermute(tiles[-1], axis, ahead))
+    index = lax.axis_index(axis)
+    tiles = jnp.stack(tiles)[(index - jnp.arange(size)) % size]
+    return in_order(tiles, dim)
 
 
 def shifted(value, axis, steps):
@@ -32,7 +49,7 @@
     block_rows = min(512, group_rows)
     score_scale = 1.0 / math.sqrt(qk_width)
     group_latent, group_rope = (
-        lax.all_gather(latent, "head", axis=0, tiled=True),
+        collect(latent, "head", 0),
         lax.all_gather(rope_keys, "head", axis=0, tiled=True),
     )
     by_heads = queries.reshape(tok_rows, groups, local_heads * qk_width)

time: 265 us -> 258 us (0.974); the launches traced: 264 us -> 254 us
  blocking collectives: 75.1 us -> 34.4 us
  waiting for transfers between devices: 17.4 us -> 46.3 us
    ppermute x0 -> x3, waiting for transfers between devices: none -> 42.1 us  [collect(): tiles.append(lax.ppermute(tiles[-1], axis, ahead))]
    all_gather x1 -> x0, blocking collectives: 41 us -> none  [shards(): lax.all_gather(latent, 'head', axis=0, tiled=True)]
    ppermute x2, waiting for transfers between devices: 15.9 us -> 0.01 us  [shifted(): lax.ppermute(value, axis, [(source, source + steps) for source in range(f...]
    all_gather x1, waiting for transfers between devices: 0.01 us -> 2.71 us  [shards(): lax.all_gather(key_weight, 'seq', axis=0, tiled=True)]
    unnamed x9 -> x10, local copies, waits for them, and re-layouts: 10.5 us -> 8.6 us
  transfers between devices with their start and end apart: 5 -> 8, of which waited for: 1 -> 3; matrix products, arithmetic and copies ran while one was open for 16% -> 17% of each run, Pallas kernels for 0% -> 0%
where the time goes in v1:
time: 258 us; the launch traced here: 254 us
  local copies, waits for them, and re-layouts  65.6 us (25%)
  matrix products  60.9 us (24%)
  waiting for transfers between devices  46.3 us (18%)
  blocking collectives  34.4 us (13%)
  other arithmetic  22.9 us (9%)
  between operations  13.6 us (5%)
  starting transfers between devices  9.79 us (4%)
    ppermute x3, waiting for transfers between devices, collect(): tiles.append(lax.ppermute(tiles[-1], axis, ahead))  42.1 us
    all_to_all x1, blocking collectives, shards(): lax.all_to_all(attended, 'head', split_axis=0, concat_axis=1, tiled=True)  28.9 us
    dot_general x2, matrix products, attend(): jnp.einsum('hij,jhd->ihd', rounded, k_values, preferred_element_type=jnp....  22.8 us
    dot_general x2, matrix products, attend(): jnp.einsum('ihd,jd->hij', q_rope, k_rope, preferred_element_type=jnp.floa...  17.9 us
    reduce_sum x2, other arithmetic, attend(): row_sum = row_sum * rescale + jnp.sum(expo, axis=2)  16.5 us
    all_to_all x1, local copies, waits for them, and re-layouts, shards(): lax.all_to_all(by_heads, 'head', split_axis=1, concat_axis=0, tiled=True)  15.6 us
    dynamic_slice x4, local copies, waits for them, and re-layouts, attend(): lax.dynamic_slice_in_dim(values_all, k_start, block_rows, 0)  15.4 us
    unnamed x10, local copies, waits for them, and re-layouts  8.6 us
  transfers between devices with their start and end apart: 8, of which 3 were waited for; matrix products, arithmetic and copies ran while one was open for 17% of the time, Pallas kernels for 0%

profile of v1, /device:TPU:24, one launch (start us, length us, event | category | flops | bytes accessed | tf_op | source)
XLA Modules:
  0.0 253.6 jit_solution(2428251457031737175)
XLA Ops:
  6.5 0.7 all-gather.5.cloned.1.call-update
  7.3 0.7 all-gather.3.cloned.1.call-update
  8.0 4.6 %copy.43 = bf16[128,12288]{0,1:T(8,128)(2,1)} copy(bf16[128,12288]{1,0:T(8,128)(2,1)} %param.8) | data formatting | bytes 6291456 | tf_op args[0]
  12.7 3.8 %all-to-all-start = ((bf16[128,4,3072]{0,2,1:T(8,128)(2,1)}), bf16[128,4,3072]{0,2,1:T(8,128)(2,1)S(1)}, u32[]{:S(2)}, u32[]{:S(2)}) async-start(bf16[128,4,3072]{0,2,1:T(8,128)(2,1)} %bitcast.66), calls=%async_computation | async-start | bytes 6291456 | tf_op jit(solution)/shard_map/all_to_all | solution.py:56
  16.5 0.5 collective-permute-start
  17.0 37.8 %collective-permute-done = bf16[128,512]{1,0:T(8,128)(2,1)S(1)} collective-permute-done((bf16[128,512]{1,0:T(8,128)(2,1)S(1)}, bf16[128,512]{1,0:T(8,128)(2,1)S(1)}, u32[]{:S(2)}, u32[]{:S(2)}) %collective-permute-start) | collective-permute-done | bytes 131104 | tf_op jit(solution)/shard_map/ppermute | solution.py:24
  54.8 5.5 %all_gather.10 = bf16[512,64]{0,1:T(8,128)(2,1)S(1)} all-gather(bf16[128,64]{0,1:T(8,128)(2,1)S(1)} %copy-done.2), channel_id=1, replica_groups=mesh['seq'=8,'head'=4] {'head'}, dimensions={0}, use_global_device_ids=true | all-gather | bytes 81920 | tf_op jit(solution)/shard_map/all_gather | solution.py:53
  60.3 3.4 %collective-permute-start.4 = (bf16[512,64]{0,1:T(8,128)(2,1)S(1)}, bf16[512,64]{0,1:T(8,128)(2,1)}, u32[]{:S(2)}, u32[]{:S(2)}) collective-permute-start(bf16[512,64]{0,1:T(8,128)(2,1)S(1)} %all_gather.10), channel_id=1, source_target_pairs={{0,4},{4,8},{8,12},{12,16},{16,20},{20,24},{24,28},{1,5},{5,9},{9,... | collective-permute-start | bytes 196616 | tf_op jit(solution)/shard_map/ppermute | solution.py:33
  63.7 0.1 collective-permute-start.2
  63.9 0.1 copy.42
  64.0 0.1 reduce
  64.1 4.3 %collective-permute-done.2 = bf16[128,512]{1,0:T(8,128)(2,1)} collective-permute-done((bf16[128,512]{1,0:T(8,128)(2,1)}, bf16[128,512]{1,0:T(8,128)(2,1)}, u32[]{:S(2)}, u32[]{:S(2)}) %collective-permute-start.2) | collective-permute-done | bytes 131104 | tf_op jit(solution)/shard_map/ppermute | solution.py:24
  68.5 1.8 pad_maximum_fusion.3
  70.3 2.4 gather_fusion
  72.7 1.9 collective-permute-start.3
  74.7 0.1 convert_reduce_fusion
  74.8 0.8 pad_maximum_fusion.4
  75.7 15.6 %copy.44 = bf16[4,128,1,3072]{1,0,3,2:T(4,128)(2,1)} copy(bf16[4,128,1,3072]{1,3,0,2:T(8,128)(2,1)S(1)} %bitcast.65) | data formatting | bytes 6291456 | tf_op jit(solution)/shard_map/all_to_all | solution.py:56
  91.3 4.0 %reshape.185 = bf16[512,16,192]{0,2,1:T(8,128)(2,1)S(1)} reshape(bf16[4,128,1,3072]{1,0,3,2:T(4,128)(2,1)} %copy.44) | data formatting | bytes 6291456 | tf_op jit(solution)/shard_map/reshape | solution.py:57
  95.3 1.5 slice.13
  96.9 1.1 slice.14
  97.9 3.9 %copy.46 = bf16[512,16,128]{2,0,1:T(8,128)(2,1)} copy(bf16[512,16,128]{0,2,1:T(8,128)(2,1)} %slice.13) | data formatting | bytes 4194304
  101.9 6.1 %convolution_convert_fusion = bf16[1024,2048]{1,0:T(8,128)(2,1)} fusion(bf16[512,2048]{1,0:T(8,128)(2,1)} %all-gather.5.cloned.1.call-done, bf16[512,512]{1,0:T(8,128)(2,1)S(1)} %bitcast.70, bf16[512,512]{1,0:T(8,128)(2,1)} %collective-permute-done.3), kind=kOutput, calls=%fused_computation.26 | convolution fusion | flops 2151677952 | bytes 7340032 | tf_op jit(solution)/shard_map/dot_general | solution.py:65
  108.0 2.7 %all-gather.3.cloned.1.call-done = bf16[512,2048]{1,0:T(8,128)(2,1)} async-done(((bf16[64,2048]{1,0:T(8,128)(2,1)}), bf16[512,2048]{1,0:T(8,128)(2,1)}) %all-gather.3.cloned.1.call-update) | async-done | bytes 2097168 | tf_op jit(solution)/shard_map/all_gather | solution.py:62
  110.7 6.1 %convolution_convert_fusion.1 = bf16[1024,2048]{1,0:T(8,128)(2,1)} fusion(bf16[512,2048]{1,0:T(8,128)(2,1)} %all-gather.3.cloned.1.call-done, bf16[512,512]{1,0:T(8,128)(2,1)S(1)} %bitcast.71, bf16[512,512]{1,0:T(8,128)(2,1)} %collective-permute-done.3), kind=kOutput, calls=%fused_computation.27 | convolution fusion | flops 2151677952 | bytes 7340032 | tf_op jit(solution)/shard_map/dot_general | solution.py:60
  116.8 87.3 %while.27 = (s32[]{:T(128)}, f32[16,512]{1,0:T(8,128)S(1)}, f32[16,512]{1,0:T(8,128)S(1)}, f32[512,16,128]{0,2,1:T(8,128)}, s32[512]{0:T(512)S(1)}, /*index=5*/s...) while((s32[]{:T(128)}, f32[16,512]{1,0:T(8,128)S(1)}, ...), condition=%wide.region_5.6_spmd.clone, body=%wide.region_2.5_spmd.clone.sunk | while | flops 2721891328 | bytes 117522640 | solution.py:124
  116.8 0.3 compare_and_fusion.2
  117.1 4.9 %constant_dynamic-slice_fusion.3 = (bf16[512,2048]{1,0:T(8,128)(2,1)}, bf16[512,2048]{1,0:T(8,128)(2,1)}) fusion(bf16[1024,2048]{1,0:T(8,128)(2,1)} %get-tuple-element.540, s32[]{:T(128)S(6)} %select_n.64, bf16[1024,2048]{1,0:T(8,128)(2,1)} %get-tuple-element.536), kind=kLoop, calls=%fused_computation.22.clone.1 | loop fusion | bytes 8388612 | tf_op jit(solution)/shard_map/while/body/eval_jaxpr/while/body/eval_jaxpr/dynamic_slice | solution.py:91
  122.0 2.9 %copy.58 = bf16[512,2048]{0,1:T(8,128)(2,1)S(1)} copy(bf16[512,2048]{1,0:T(8,128)(2,1)} %get-tuple-element.492) | data formatting | bytes 4194304 | tf_op jit(solution)/shard_map/while/body/eval_jaxpr/while/body/eval_jaxpr/dynamic_slice | solution.py:87
  124.8 4.0 %fusion.43 = f32[16,512,512]{2,1,0:T(8,128)S(1)} fusion(bf16[512,16,128]{0,2,1:T(8,128)(2,1)S(1)} %bitcast.64, bf16[512,16,128]{2,0,1:T(8,128)(2,1)} %get-tuple-element.537), kind=kOutput, calls=%fused_computation.44.clone.1 | convolution fusion | flops 1073741824 | bytes 20971520 | tf_op jit(solution)/shard_map/while/body/eval_jaxpr/while/body/eval_jaxpr/ihd,jhd->hij/dot_general | solution.py:96
  128.8 9.0 %fusion.44 = (f32[16,512]{1,0:T(8,128)S(1)}, f32[16,512,512]{1,2,0:T(8,128)}) fusion(bf16[512,16,64]{0,2,1:T(8,128)(2,1)} %get-tuple-element.539, bf16[1024,64]{0,1:T(8,128)(2,1)S(1)} %get-tuple-element.538, s32[]{:T(128)S(6)} %select_n.64, f32[16,512,512]{2,1,0:T(8,128)S(1)} %fusion.43, pred[512,512]{0,1:T(8,128)(4,1)S(1)} %compare_and_fusion.2), kind=kOutput, calls=%fused_computation.43.clone.1 | convolution fusion | flops 553639936 | bytes 34963460 | tf_op jit(solution)/shard_map/while/body/eval_jaxpr/while/body/eval_jaxpr/ihd,jd->hij/dot_general | solution.py:99
  137.8 2.9 %copy.59 = bf16[512,2048]{0,1:T(8,128)(2,1)S(1)} copy(bf16[512,2048]{1,0:T(8,128)(2,1)} %get-tuple-element.498) | data formatting | bytes 4194304 | tf_op jit(solution)/shard_map/while/body/eval_jaxpr/while/body/eval_jaxpr/dynamic_slice | solution.py:91
  140.7 10.8 %bitcast_add_fusion.3 = f32[512,16,128]{0,2,1:T(8,128)} fusion(f32[512,16,128]{0,2,1:T(8,128)} %get-tuple-element.518, bf16[512,16,128]{0,2,1:T(8,128)(2,1)S(1)} %bitcast.63, f32[16,512,512]{1,2,0:T(8,128)} %get-tuple-element.497, f32[16,512]{1,0:T(8,128)S(1)} %get-tuple-element.531, f32[512,16]{0,1:T(8,128)S(1)} %get-tuple-element.499, ...), kind=kOutput, calls=%fused_computation.10.clone.1 | convolution fusion | flops 1085276160 | bytes 27328512 | tf_op jit(solution)/shard_map/while/body/eval_jaxpr/while/body/eval_jaxpr/hij,jhd->ihd/dot_general | solution.py:110
  151.5 8.3 %fusion.46 = f32[16,512]{1,0:T(8,128)S(1)} fusion(f32[16,512,512]{1,2,0:T(8,128)} %get-tuple-element.497, f32[16,512]{1,0:T(8,128)S(1)} %get-tuple-element.531), kind=kLoop, calls=%fused_computation.7.clone.1 | loop fusion | flops 8380416 | bytes 16842752 | tf_op jit(solution)/shard_map/while/body/eval_jaxpr/while/body/eval_jaxpr/reduce_sum | solution.py:108
  159.9 0.3 compare_and_fusion.2
  160.2 4.9 %constant_dynamic-slice_fusion.3 = (bf16[512,2048]{1,0:T(8,128)(2,1)}, bf16[512,2048]{1,0:T(8,128)(2,1)}) fusion(bf16[1024,2048]{1,0:T(8,128)(2,1)} %get-tuple-element.540, s32[]{:T(128)S(6)} %select_n.64, bf16[1024,2048]{1,0:T(8,128)(2,1)} %get-tuple-element.536), kind=kLoop, calls=%fused_computation.22.clone.1 | loop fusion | bytes 8388612 | tf_op jit(solution)/shard_map/while/body/eval_jaxpr/while/body/eval_jaxpr/dynamic_slice | solution.py:91
  165.1 2.9 %copy.58 = bf16[512,2048]{0,1:T(8,128)(2,1)S(1)} copy(bf16[512,2048]{1,0:T(8,128)(2,1)} %get-tuple-element.492) | data formatting | bytes 4194304 | tf_op jit(solution)/shard_map/while/body/eval_jaxpr/while/body/eval_jaxpr/dynamic_slice | solution.py:87
  167.9 4.0 %fusion.43 = f32[16,512,512]{2,1,0:T(8,128)S(1)} fusion(bf16[512,16,128]{0,2,1:T(8,128)(2,1)S(1)} %bitcast.64, bf16[512,16,128]{2,0,1:T(8,128)(2,1)} %get-tuple-element.537), kind=kOutput, calls=%fused_computation.44.clone.1 | convolution fusion | flops 1073741824 | bytes 20971520 | tf_op jit(solution)/shard_map/while/body/eval_jaxpr/while/body/eval_jaxpr/ihd,jhd->hij/dot_general | solution.py:96
  171.9 9.0 %fusion.44 = (f32[16,512]{1,0:T(8,128)S(1)}, f32[16,512,512]{1,2,0:T(8,128)}) fusion(bf16[512,16,64]{0,2,1:T(8,128)(2,1)} %get-tuple-element.539, bf16[1024,64]{0,1:T(8,128)(2,1)S(1)} %get-tuple-element.538, s32[]{:T(128)S(6)} %select_n.64, f32[16,512,512]{2,1,0:T(8,128)S(1)} %fusion.43, pred[512,512]{0,1:T(8,128)(4,1)S(1)} %compare_and_fusion.2), kind=kOutput, calls=%fused_computation.43.clone.1 | convolution fusion | flops 553639936 | bytes 34963460 | tf_op jit(solution)/shard_map/while/body/eval_jaxpr/while/body/eval_jaxpr/ihd,jd->hij/dot_general | solution.py:99
  180.9 2.9 %copy.59 = bf16[512,2048]{0,1:T(8,128)(2,1)S(1)} copy(bf16[512,2048]{1,0:T(8,128)(2,1)} %get-tuple-element.498) | data formatting | bytes 4194304 | tf_op jit(solution)/shard_map/while/body/eval_jaxpr/while/body/eval_jaxpr/dynamic_slice | solution.py:91
  183.8 12.0 %bitcast_add_fusion.3 = f32[512,16,128]{0,2,1:T(8,128)} fusion(f32[512,16,128]{0,2,1:T(8,128)} %get-tuple-element.518, bf16[512,16,128]{0,2,1:T(8,128)(2,1)S(1)} %bitcast.63, f32[16,512,512]{1,2,0:T(8,128)} %get-tuple-element.497, f32[16,512]{1,0:T(8,128)S(1)} %get-tuple-element.531, f32[512,16]{0,1:T(8,128)S(1)} %get-tuple-element.499, ...), kind=kOutput, calls=%fused_computation.10.clone.1 | convolution fusion | flops 1085276160 | bytes 27328512 | tf_op jit(solution)/shard_map/while/body/eval_jaxpr/while/body/eval_jaxpr/hij,jhd->ihd/dot_general | solution.py:110
  195.8 8.3 %fusion.46 = f32[16,512]{1,0:T(8,128)S(1)} fusion(f32[16,512,512]{1,2,0:T(8,128)} %get-tuple-element.497, f32[16,512]{1,0:T(8,128)S(1)} %get-tuple-element.531), kind=kLoop, calls=%fused_computation.7.clone.1 | loop fusion | flops 8380416 | bytes 16842752 | tf_op jit(solution)/shard_map/while/body/eval_jaxpr/while/body/eval_jaxpr/reduce_sum | solution.py:108
  204.1 2.8 %divide_convert_fusion = bf16[512,16,128]{0,2,1:T(8,128)(2,1)S(1)} fusion(f32[512,16,128]{0,2,1:T(8,128)} %get-tuple-element.292, f32[512,16]{0,1:T(8,128)S(1)} %bitcast.68), kind=kLoop, calls=%fused_computation.25 | loop fusion | flops 2097152 | bytes 6324224 | tf_op jit(solution)/shard_map/while/body/eval_jaxpr/convert_element_type | solution.py:126
  206.9 2.0 reshape.197
  208.9 3.0 %copy.53 = bf16[4,128,2048]{2,1,0:T(8,128)(2,1)S(1)} copy(bf16[4,128,2048]{1,0,2:T(4,128)(2,1)} %reshape.197) | data formatting | bytes 4194304 | tf_op jit(solution)/shard_map/while/body/eval_jaxpr/convert_element_type | solution.py:126
  211.9 28.9 %all_to_all.31 = bf16[4,128,2048]{2,1,0:T(8,128)(2,1)} all-to-all(bf16[4,128,2048]{2,1,0:T(8,128)(2,1)S(1)} %copy.53), channel_id=1, replica_groups=mesh['seq'=8,'head'=4] {'head'}, dimensions={0} | all-to-all | bytes 4194304 | tf_op jit(solution)/shard_map/all_to_all | solution.py:130
  240.8 3.0 %copy.49 = bf16[4,128,2048]{1,2,0:T(8,128)(2,1)S(1)} copy(bf16[4,128,2048]{2,1,0:T(8,128)(2,1)} %all_to_all.31) | data formatting | bytes 4194304 | tf_op jit(solution)/shard_map/all_to_all | solution.py:130
  243.8 2.9 %copy.50 = bf16[128,8192]{1,0:T(8,128)(2,1)} copy(bf16[128,8192]{0,1:T(8,128)(2,1)S(1)} %bitcast.67) | data formatting | bytes 4194304 | tf_op jit(solution)/shard_map/all_to_all | solution.py:130
  (36 shorter events, 0.4 us)
Async XLA Ops:
  6.5 95.4 %all-gather.5.cloned.1.call-start = ((), (), s32[]{:S(2)}) async-start(), calls=%async_computation.3 | async-start | bytes 2359296 | tf_op jit(solution)/shard_map/all_gather | solution.py:67
  7.3 103.4 %all-gather.3.cloned.1.call-start = ((), (), s32[]{:S(2)}) async-start(), calls=%async_computation.2 | async-start | bytes 2359296 | tf_op jit(solution)/shard_map/all_gather | solution.py:62
  12.6 3.9 %copy-start.1 = (bf16[128,512]{1,0:T(8,128)(2,1)S(1)}, bf16[128,512]{1,0:T(8,128)(2,1)}, u32[]{:S(2)}) copy-start(bf16[128,512]{1,0:T(8,128)(2,1)} %param.9) | copy-start | bytes 393220
  12.6 42.1 %copy-start.2 = (bf16[128,64]{0,1:T(8,128)(2,1)S(1)}, bf16[128,64]{0,1:T(8,128)(2,1)}, u32[]{:S(2)}) copy-start(bf16[128,64]{0,1:T(8,128)(2,1)} %param.10) | copy-start | bytes 49156
  12.7 51.2 %copy-start.3 = (s32[32]{0:T(128)S(1)}, s32[32]{0:T(128)}, u32[]{:S(2)}) copy-start(s32[32]{0:T(128)} %param.13) | copy-start | bytes 388
  12.7 63.0 %all-to-all-start = ((bf16[128,4,3072]{0,2,1:T(8,128)(2,1)}), bf16[128,4,3072]{0,2,1:T(8,128)(2,1)S(1)}, u32[]{:S(2)}, u32[]{:S(2)}) async-start(bf16[128,4,3072]{0,2,1:T(8,128)(2,1)} %bitcast.66), calls=%async_computation | async-start | bytes 6291456 | tf_op jit(solution)/shard_map/all_to_all | solution.py:56
  16.5 38.3 %collective-permute-start = (bf16[128,512]{1,0:T(8,128)(2,1)S(1)}, bf16[128,512]{1,0:T(8,128)(2,1)S(1)}, u32[]{:S(2)}, u32[]{:S(2)}) collective-permute-start(bf16[128,512]{1,0:T(8,128)(2,1)S(1)} %copy-done.1), channel_id=1, source_target_pairs={{0,1},{1,2},{2,3},{3,0},{4,5},{5,6},{6,7},{7,4},{8,9},{9,10},{10,1... | collective-permute-start | bytes 393224 | tf_op jit(solution)/shard_map/ppermute | solution.py:24
  54.8 8.9 %collective-permute-start.1 = (bf16[128,512]{1,0:T(8,128)(2,1)S(1)}, bf16[128,512]{1,0:T(8,128)(2,1)}, u32[]{:S(2)}, u32[]{:S(2)}) collective-permute-start(bf16[128,512]{1,0:T(8,128)(2,1)S(1)} %collective-permute-done), channel_id=1, source_target_pairs={{0,1},{1,2},{2,3},{3,0},{4,5},{5,6},{6,7},{7,4},{8,9},{9,10},{10,1... | collective-permute-start | bytes 393224 | tf_op jit(solution)/shard_map/ppermute | solution.py:24
  60.3 14.5 %collective-permute-start.4 = (bf16[512,64]{0,1:T(8,128)(2,1)S(1)}, bf16[512,64]{0,1:T(8,128)(2,1)}, u32[]{:S(2)}, u32[]{:S(2)}) collective-permute-start(bf16[512,64]{0,1:T(8,128)(2,1)S(1)} %all_gather.10), channel_id=1, source_target_pairs={{0,4},{4,8},{8,12},{12,16},{16,20},{20,24},{24,28},{1,5},{5,9},{9,... | collective-permute-start | bytes 196616 | tf_op jit(solution)/shard_map/ppermute | solution.py:33
  63.7 4.8 %collective-permute-start.2 = (bf16[128,512]{1,0:T(8,128)(2,1)}, bf16[128,512]{1,0:T(8,128)(2,1)}, u32[]{:S(2)}, u32[]{:S(2)}) collective-permute-start(bf16[128,512]{1,0:T(8,128)(2,1)} %collective-permute-done.1), channel_id=1, source_target_pairs={{0,1},{1,2},{2,3},{3,0},{4,5},{5,6},{6,7},{7,4},{8,9},{9,10},{10,1... | collective-permute-start | bytes 393224 | tf_op jit(solution)/shard_map/ppermute | solution.py:24
  72.7 29.2 %collective-permute-start.3 = (bf16[512,512]{1,0:T(8,128)(2,1)}, bf16[512,512]{1,0:T(8,128)(2,1)}, u32[]{:S(2)}, u32[]{:S(2)}) collective-permute-start(bf16[512,512]{1,0:T(8,128)(2,1)} %bitcast.69), channel_id=1, source_target_pairs={{0,4},{4,8},{8,12},{12,16},{16,20},{20,24},{24,28},{1,5},{5,9},{9,... | collective-permute-start | bytes 1572872 | tf_op jit(solution)/shard_map/ppermute | solution.py:33
  97.9 4.0 %copy-start = (bf16[4,128,512]{2,1,0:T(8,128)(2,1)S(1)}, bf16[4,128,512]{2,1,0:T(8,128)(2,1)}, u32[]{:S(2)}) copy-start(bf16[4,128,512]{2,1,0:T(8,128)(2,1)} %gather_fusion) | copy-start | bytes 1572868
Sparse Core Ops, SparseCore 0:
  9.5 48.5 all-gather.4
  60.2 50.4 all-gather.2
